TPU v7x, 512 devices: a whole 4x4x16 slice. The times are simulated.
512 devices in a mesh: bytes: 16 (over z), ctx: 8 (over x, core), tp: 4 (over y).
Axes of the slice: x: 4, y: 4, z: 16, core: 2. Of those that a mesh axis runs over, the one named last changes fastest.
Arguments:
- byte_values_sequence: int32 [24576], P(('bytes', 'ctx')), may hold values from 0 to 255
- offsets: int32 [24576], P(('bytes', 'ctx')), may hold values from 0 to 168, as said below
- byte_table: bfloat16 [256, 1024], replicated, may hold values from -6 to 6
- byte_query: bfloat16 [1024, 1024], P(None, 'tp'), may hold values from -1 to 1
- byte_key: bfloat16 [1024, 1024], P(None, 'tp'), may hold values from -16 to 16
- byte_value: bfloat16 [1024, 1024], P(None, 'tp'), may hold values from -0.1875 to 0.1875
- latent_query: bfloat16 [1024, 4096], P(None, ('ctx', 'tp')), may hold values from -1 to 1
- latent_key: bfloat16 [1024, 4096], P(None, ('ctx', 'tp')), may hold values from -16 to 16
- latent_value: bfloat16 [1024, 4096], P(None, ('ctx', 'tp')), may hold values from -0.1875 to 0.1875
- decode_weight: bfloat16 [4096, 1024], P(('ctx', 'tp')), may hold values from -1 to 1
Outputs:
- byte_output: bfloat16 [24576, 1024], P(('bytes', 'ctx'), 'tp')
Inputs may be any that keep to these rules, and one draw needn't show every extreme that they name: offsets[i] is 0 where a patch starts and offsets[i - 1] + 1 elsewhere; the first byte of every device's 192 bytes starts a patch; one device's bytes hold 24 to 72 patch starts and the bytes of the devices of one index of bytes hold at most 384; both most values are reached in every draw.
All inputs are finite; a program needn't handle non-finite values.
Results may differ from a plain program's by a relative error of at most 0.017.
Values may be sent and summed in bfloat16 or wider, within the bound.
No kernel may reach another device: no remote copies, remote signals or barrier semaphores. Data moves between devices by JAX's collectives and lax.ppermute only.
A program may use at most 64 MiB of HBM per device.

v0:
```python
import math
import jax
import jax.numpy as jnp
from jax import lax
from jax.sharding import PartitionSpec as P

DB = 1024
HEADS_B = 16
HEAD_L = 128
EPSILON = 1e-06
NEGATIVE = -1e30
FARAWAY = 1 << 30


def from_behind(value, axis, steps):
    count = lax.axis_size(axis)
    first, last = (max(0, -steps), min(count, count - steps))
    return lax.ppermute(value, axis, [(source, source + steps) for source in range(first, last)])


def copy_for_each(array, axis):
    copies = jnp.broadcast_to(array, (lax.axis_size(axis), *array.shape))
    return lax.all_to_all(copies, axis, split_axis=0, concat_axis=0, tiled=True)


def joined_along(tiles, dim):
    tiles = jnp.moveaxis(tiles, 0, dim)
    lengths = tiles.shape
    return tiles.reshape(*lengths[:dim], lengths[dim] * lengths[dim + 1], *lengths[dim + 2 :])


def collect(array, axis, dim):
    tiles = copy_for_each(array, axis)
    return joined_along(tiles, dim)


def sent_together(arrays, axis, dim, along):
    widths = [a.shape[along] for a in arrays]
    both = jnp.concatenate(arrays, axis=along)
    filled = lax.all_gather(both, axis, axis=dim, tiled=True)
    return tuple(jnp.split(filled, [sum(widths[:k]) for k in range(1, len(widths))], axis=along))


def cut_along(array, dim, count):
    before, after = (array.shape[:dim], array.shape[dim + 1 :])
    return jnp.moveaxis(array.reshape(*before, count, -1, *after), dim, 0)


def sent_and_summed(array, axis, dim):
    tiles = cut_along(array, dim, lax.axis_size(axis))
    arrived = lax.all_to_all(tiles, axis, split_axis=0, concat_axis=0, tiled=True)
    return arrived.astype(jnp.float32).sum(axis=0)


def norm_rows(values):
    values = values.astype(jnp.float32)
    return values * lax.rsqrt(jnp.mean(values * values, axis=-1, keepdims=True) + EPSILON)


def project(inputs, weight):
    return jnp.dot(inputs, weight, preferred_element_type=jnp.float32).astype(jnp.bfloat16)


def byte_project(byte_values_sequence, byte_table, weights):
    onehot = (
        byte_values_sequence[:, None] == jnp.arange(byte_table.shape[0], dtype=jnp.int32)[None, :]
    ).astype(jnp.bfloat16)
    embedded = jnp.dot(onehot, byte_table, preferred_element_type=jnp.float32)
    normed = norm_rows(embedded).astype(jnp.bfloat16)
    return tuple((project(normed, weight) for weight in weights))


def per_device(
    byte_values_sequence,
    offsets,
    byte_table,
    byte_query,
    byte_key,
    byte_value,
    latent_query,
    latent_key,
    latent_value,
    decode_weight,
):
    row_count = byte_values_sequence.shape[0]
    channels = byte_query.shape[1]
    heads_here = HEADS_B * channels // DB
    head_feature_width = channels // heads_here
    ctx_count = lax.axis_size("ctx")
    tp_count = lax.axis_size("tp")
    slot_cap = 3 * row_count // 8
    block_index = lax.axis_index(("bytes", "ctx"))
    byte_window_queries, byte_window_keys, values_b = byte_project(
        byte_values_sequence, byte_table, (byte_query, byte_key, byte_value)
    )
    earlier_ids = from_behind(byte_values_sequence, ("bytes", "ctx"), 1)
    keys_e, values_e = byte_project(earlier_ids, byte_table, (byte_key, byte_value))
    keys_w = jnp.concatenate([keys_e, byte_window_keys], axis=0).reshape(
        2 * row_count, heads_here, head_feature_width
    )
    values_w = jnp.concatenate([values_e, values_b], axis=0).reshape(
        2 * row_count, heads_here, head_feature_width
    )
    queries_w = byte_window_queries.reshape(row_count, heads_here, head_feature_width)
    query_pos = jnp.arange(row_count, dtype=jnp.int32)[:, None]
    key_pos = jnp.arange(2 * row_count, dtype=jnp.int32)[None, :]
    allowed_b = (
        (key_pos > query_pos)
        & (key_pos <= query_pos + row_count)
        & ((key_pos >= row_count) | (block_index > 0))
    )
    scores_b = jnp.einsum(
        "qhd,khd->hqk", queries_w, keys_w, preferred_element_type=jnp.float32
    ) / math.sqrt(head_feature_width)
    scores_b = jnp.where(allowed_b[None], scores_b, NEGATIVE)
    highest_b = jnp.max(scores_b, axis=-1, keepdims=True)
    weights_b = jnp.where(allowed_b[None], jnp.exp(scores_b - highest_b), 0.0)
    totals_b = jnp.sum(weights_b, axis=-1)
    blended = jnp.einsum(
        "hqk,khd->qhd", weights_b.astype(jnp.bfloat16), values_w, preferred_element_type=jnp.float32
    )
    encoded = (blended / totals_b.T[:, :, None]).reshape(row_count, channels).astype(jnp.bfloat16)
    starts = (offsets == 0).astype(jnp.int32)
    local_patch = jnp.cumsum(starts) - 1
    members = local_patch[None, :] == jnp.arange(slot_cap, dtype=jnp.int32)[:, None]
    patch_sums = jnp.dot(members.astype(jnp.bfloat16), encoded, preferred_element_type=jnp.float32)
    lengths = jnp.sum(members.astype(jnp.float32), axis=1)
    pooled = (patch_sums / jnp.maximum(lengths, 1.0)[:, None]).astype(jnp.bfloat16)
    gathered, patch_counts = (
        collect(pooled, ("ctx", "tp"), 0),
        collect(local_patch[-1:] + 1, ("ctx", "tp"), 0),
    )
    features = gathered.reshape(ctx_count, tp_count, slot_cap, channels).transpose(0, 2, 1, 3)
    features = features.reshape(ctx_count * slot_cap, tp_count * channels)
    patch_counts = patch_counts.reshape(ctx_count, tp_count)[:, 0]
    slot_ids = jnp.arange(slot_cap, dtype=jnp.int32)
    block_ids = lax.axis_index("bytes") * ctx_count + jnp.arange(ctx_count, dtype=jnp.int32)
    positions = jnp.where(
        slot_ids[None, :] < patch_counts[:, None],
        block_ids[:, None] * slot_cap + slot_ids[None, :],
        FARAWAY,
    ).reshape(-1)
    capacity = ctx_count * row_count // 4
    running = jnp.cumsum((positions < FARAWAY).astype(jnp.int32))
    targets = jnp.arange(capacity, dtype=jnp.int32)
    chosen = jnp.minimum(jnp.searchsorted(running, targets + 1), running.shape[0] - 1)
    features = features[chosen]
    positions = jnp.where(targets < running[-1], positions[chosen], FARAWAY)
    latent_in = norm_rows(features).astype(jnp.bfloat16)
    queries_l = project(latent_in, latent_query)
    keys_l = project(latent_in, latent_key)
    values_l = project(latent_in, latent_value)
    query_rows = queries_l.shape[0]
    heads_latent = queries_l.shape[1] // HEAD_L
    queries_h = queries_l.reshape(query_rows, heads_latent, HEAD_L)
    initial = (
        jnp.full((heads_latent, query_rows), NEGATIVE, jnp.float32),
        jnp.zeros((heads_latent, query_rows), jnp.float32),
        jnp.zeros((query_rows, heads_latent, HEAD_L), jnp.float32),
    )
    running_state = initial
    keys_p, values_p, places_p = (
        *sent_together((keys_l, values_l), "bytes", 0, 1),
        lax.all_gather(positions, "bytes", axis=0, tiled=True),
    )
    span_rows = keys_p.shape[0]

    def attend_block(state, step_index):
        highest, totals, accumulated = state
        keys_s = lax.dynamic_slice_in_dim(keys_p, step_index * query_rows, query_rows, 0).reshape(
            query_rows, heads_latent, HEAD_L
        )
        values_s = lax.dynamic_slice_in_dim(
            values_p, step_index * query_rows, query_rows, 0
        ).reshape(query_rows, heads_latent, HEAD_L)
        places = lax.dynamic_slice_in_dim(places_p, step_index * query_rows, query_rows, 0)
        attention_scores = jnp.einsum(
            "qhd,khd->hqk", queries_h, keys_s, preferred_element_type=jnp.float32
        ) / math.sqrt(HEAD_L)
        allowed = (places[None, :] <= positions[:, None])[None]
        highest_new = jnp.maximum(
            highest, jnp.max(jnp.where(allowed, attention_scores, NEGATIVE), axis=-1)
        )
        factor = jnp.exp(highest - highest_new)
        weights = jnp.where(allowed, jnp.exp(attention_scores - highest_new[:, :, None]), 0.0)
        totals = totals * factor + jnp.sum(weights, axis=-1)
        mixed_in = jnp.einsum(
            "hqk,khd->qhd",
            weights.astype(jnp.bfloat16),
            values_s,
            preferred_element_type=jnp.float32,
        )
        accumulated = accumulated * factor.T[:, :, None] + mixed_in
        return ((highest_new, totals, accumulated), None)

    running_state, _ = lax.scan(
        attend_block, running_state, jnp.arange(span_rows // query_rows, dtype=jnp.int32)
    )
    highest_l, totals_l, accumulated_l = running_state
    latent_out = (
        (accumulated_l / totals_l.T[:, :, None])
        .reshape(query_rows, heads_latent * HEAD_L)
        .astype(jnp.bfloat16)
    )
    shares = sent_and_summed(
        jnp.dot(latent_out, decode_weight, preferred_element_type=jnp.float32).astype(jnp.bfloat16),
        ("ctx", "tp"),
        0,
    )
    summed = collect(shares.astype(jnp.bfloat16), ("ctx", "tp"), 0).astype(shares.dtype)
    before = jnp.sum(
        jnp.where(jnp.arange(ctx_count, dtype=jnp.int32) < lax.axis_index("ctx"), patch_counts, 0)
    )
    mine = lax.dynamic_slice_in_dim(summed, lax.axis_index("tp") * channels, channels, 1)
    decoded_bytes = mine[before + local_patch]
    return (encoded.astype(jnp.float32) + decoded_bytes).astype(jnp.bfloat16)


def solution(mesh):
    return jax.shard_map(
        per_device,
        mesh=mesh,
        in_specs=(
            P(("bytes", "ctx")),
            P(("bytes", "ctx")),
            P(),
            P(None, "tp"),
            P(None, "tp"),
            P(None, "tp"),
            P(None, ("ctx", "tp")),
            P(None, ("ctx", "tp")),
            P(None, ("ctx", "tp")),
            P(("ctx", "tp"), None),
        ),
        out_specs=P(("bytes", "ctx"), "tp"),
        check_vma=False,
    )
```

profile of v0, /device:TPU:1, one launch (start us, length us, event | category | flops | bytes accessed | tf_op | source)
XLA Modules:
  0.0 257.1 jit_solution(15806933889242681807)
XLA Ops:
  6.5 4.6 %collective-permute-start = (s32[192]{0:T(256)}, s32[192]{0:T(256)S(1)}, u32[]{:S(2)}, u32[]{:S(2)}) collective-permute-start(s32[192]{0:T(256)} %param.14), channel_id=1, source_target_pairs={{0,4},{4,8},{8,12},{12,16},{16,20},{20,24},{24,28},{28,32},{32,36}... | collective-permute-start | bytes 2312 | tf_op jit(solution)/shard_map/ppermute | solution.py:18
  11.2 0.7 broadcast_compare_fusion.1
  14.9 7.3 %all-to-all-start = ((s32[32,1,1]{2,1,0:T(1,128)}), s32[32,1,1]{2,1,0:T(1,128)S(1)}, u32[]{:S(2)}, u32[]{:S(2)}) async-start(s32[32,1,1]{2,1,0:T(1,128)} %broadcast_in_dim.111), calls=%async_computation | async-start | bytes 32768 | tf_op jit(solution)/shard_map/all_to_all | solution.py:23
  22.3 1.1 multiply_reduce_fusion
  24.8 0.9 convolution_convert_fusion.7
  26.6 2.6 %all-to-all-done = s32[32,1,1]{2,1,0:T(1,128)S(1)} async-done(((s32[32,1,1]{2,1,0:T(1,128)}), s32[32,1,1]{2,1,0:T(1,128)S(1)}, u32[]{:S(2)}, u32[]{:S(2)}) %all-to-all-start) | async-done | bytes 160 | tf_op jit(solution)/shard_map/all_to_all | solution.py:23
  32.2 0.7 fusion.53
  33.0 1.3 fusion.25
  36.1 1.1 broadcast_in_dim.118
  37.2 4.8 %all-to-all-start.1 = ((bf16[32,72,256]{2,1,0:T(8,128)(2,1)}), bf16[32,72,256]{2,1,0:T(8,128)(2,1)S(1)}, u32[]{:S(2)}, u32[]{:S(2)}) async-start(bf16[32,72,256]{2,1,0:T(8,128)(2,1)} %broadcast_in_dim.118), calls=%async_computation.1 | async-start | bytes 2359296 | tf_op jit(solution)/shard_map/all_to_all | solution.py:23
  42.0 19.8 %while.39 = (s32[]{:T(128)}, u32[384]{0:T(512)S(1)}, u32[384]{0:T(512)S(1)}, s32[576]{0:T(1024)S(1)}, s32[]{:T(128)}, /*index=5*/s32[]{:T(128)}, s32[]{}) while((s32[]{:T(128)}, u32[384]{0:T(512)S(1)}, u32[384]{0:T(512)S(1)}, s32[576]{0:T(1024)S(1)}, s32[]{:T(128)}, /*index=5*/s32[]{:T(128)}, s32[]{}) %tuple.72), condition=%wide.region_10.11_spmd.clone, body=%wide.region_9.10_spmd.clone.sunk | while | flops 8324 | bytes 29541 | solution.py:146
  42.1 1.9 gather_fusion
  44.1 1.9 gather_fusion
  46.0 1.9 gather_fusion
  48.0 1.9 gather_fusion
  50.0 1.9 gather_fusion
  52.0 1.9 gather_fusion
  54.0 1.9 gather_fusion
  56.0 1.9 gather_fusion
  57.9 1.9 gather_fusion
  59.9 1.9 gather_fusion
  62.7 2.1 gather_fusion.2
  66.2 0.7 pad_maximum_fusion.2
  66.9 1.9 gather_fusion.1
  70.1 29.0 %all-gather = s32[16,1,384]{2,1,0:T(1,128)S(1)} all-gather(s32[1,1,384]{2,1,0:T(1,128)S(1)} %reshape.249), channel_id=1, replica_groups=mesh['bytes'=16,'ctx'=8,'tp'=4] {'bytes'}, dimensions={0}, use_global_device_ids=true | all-gather | bytes 26112 | tf_op jit(solution)/shard_map/all_gather | solution.py:164
  99.5 38.2 %all-gather.3.cloned.1.call-done = bf16[6144,256]{0,1:T(8,128)(2,1)} async-done(((bf16[384,256]{0,1:T(8,128)(2,1)}), bf16[6144,256]{0,1:T(8,128)(2,1)}) %all-gather.3.cloned.1.call-update) | async-done | bytes 3145744 | tf_op jit(solution)/shard_map/all_gather | solution.py:40
  137.7 3.3 %fusion.52 = (bf16[6144,128]{0,1:T(8,128)(2,1)S(1)}, bf16[6144,128]{0,1:T(8,128)(2,1)}) fusion(bf16[6144,256]{0,1:T(8,128)(2,1)} %all-gather.3.cloned.1.call-done), kind=kLoop, calls=%fused_computation.120 | loop fusion | bytes 6291456 | tf_op jit(solution)/shard_map/split | solution.py:41
  141.0 51.5 %while.40 = (s32[]{:T(128)}, f32[1,384]{1,0:T(1,128)S(1)}, f32[1,384]{1,0:T(1,128)S(1)}, f32[384,1,128]{0,2,1:T(8,128)S(1)}, s32[16]{0:T(128)S(1)}, /*index=5*/s...) while((s32[]{:T(128)}, f32[1,384]{1,0:T(1,128)S(1)}, ...), condition=%wide.region_15.16_spmd.clone, body=%wide.region_12.15_spmd.clone.sunk | while | flops 77416712 | bytes 2498263 | solution.py:196
  142.4 1.2 fusion.84
  144.2 0.7 dynamic_slice.34
  145.7 1.2 fusion.84
  147.4 0.7 dynamic_slice.34
  148.9 1.2 fusion.84
  150.7 0.7 dynamic_slice.34
  152.1 1.2 fusion.84
  153.9 0.7 dynamic_slice.34
  155.3 1.2 fusion.84
  157.1 0.7 dynamic_slice.34
  158.5 1.2 fusion.84
  160.3 0.7 dynamic_slice.34
  161.8 1.2 fusion.84
  163.5 0.7 dynamic_slice.34
  165.0 1.2 fusion.84
  166.7 0.7 dynamic_slice.34
  168.2 1.2 fusion.84
  170.0 0.7 dynamic_slice.34
  171.4 1.2 fusion.84
  173.2 0.7 dynamic_slice.34
  174.6 1.2 fusion.84
  176.4 0.7 dynamic_slice.34
  177.8 1.2 fusion.84
  179.6 0.7 dynamic_slice.34
  181.1 1.2 fusion.84
  182.8 0.7 dynamic_slice.34
  184.3 1.2 fusion.84
  186.0 0.7 dynamic_slice.34
  187.5 1.2 fusion.84
  189.3 0.7 dynamic_slice.34
  190.7 1.2 fusion.84
  193.1 33.0 %all_to_all.21 = bf16[32,12,1024]{2,1,0:T(8,128)(2,1)S(1)} all-to-all(bf16[32,12,1024]{2,1,0:T(8,128)(2,1)S(1)} %reshape.208), channel_id=1, replica_groups=mesh['bytes'=16,'ctx'=8,'tp'=4] {'ctx','tp'}, dimensions={0} | all-to-all | bytes 1572864 | tf_op jit(solution)/shard_map/all_to_all | solution.py:51
  226.3 1.1 broadcast_in_dim.119
  227.4 4.8 %all-to-all-start.3 = ((bf16[32,12,1024]{2,1,0:T(8,128)(2,1)}), bf16[32,12,1024]{2,1,0:T(8,128)(2,1)S(1)}, u32[]{:S(2)}, u32[]{:S(2)}) async-start(bf16[32,12,1024]{2,1,0:T(8,128)(2,1)} %broadcast_in_dim.119), calls=%async_computation.3 | async-start | bytes 2097152 | tf_op jit(solution)/shard_map/all_to_all | solution.py:23
  233.6 14.9 %all-to-all-done.3 = bf16[32,12,1024]{2,1,0:T(8,128)(2,1)S(1)} async-done(((bf16[32,12,1024]{2,1,0:T(8,128)(2,1)}), bf16[32,12,1024]{2,1,0:T(8,128)(2,1)S(1)}, u32[]{:S(2)}, u32[]{:S(2)}) %all-to-all-start.3) | async-done | bytes 786464 | tf_op jit(solution)/shard_map/all_to_all | solution.py:23
  248.7 0.9 gather_fusion.3
  (268 shorter events, 27.2 us)
Async XLA Ops:
  6.5 15.8 %copy-start = (bf16[256,1024]{1,0:T(8,128)(2,1)S(1)}, bf16[256,1024]{1,0:T(8,128)(2,1)}, u32[]{:S(2)}) copy-start(bf16[256,1024]{1,0:T(8,128)(2,1)} %param.16) | copy-start | bytes 1572868
  6.5 24.7 %collective-permute-start = (s32[192]{0:T(256)}, s32[192]{0:T(256)S(1)}, u32[]{:S(2)}, u32[]{:S(2)}) collective-permute-start(s32[192]{0:T(256)} %param.14), channel_id=1, source_target_pairs={{0,4},{4,8},{8,12},{12,16},{16,20},{20,24},{24,28},{28,32},{32,36}... | collective-permute-start | bytes 2312 | tf_op jit(solution)/shard_map/ppermute | solution.py:18
  12.5 0.6 copy-start.13
  13.1 10.4 %copy-start.17 = (s32[192]{0:T(256)}, s32[192]{0:T(256)S(1)}, u32[]{:S(2)}) copy-start(s32[192]{0:T(256)S(1)} %slice_add_fusion) | copy-start | bytes 2308
  14.9 14.2 %all-to-all-start = ((s32[32,1,1]{2,1,0:T(1,128)}), s32[32,1,1]{2,1,0:T(1,128)S(1)}, u32[]{:S(2)}, u32[]{:S(2)}) async-start(s32[32,1,1]{2,1,0:T(1,128)} %broadcast_in_dim.111), calls=%async_computation | async-start | bytes 32768 | tf_op jit(solution)/shard_map/all_to_all | solution.py:23
  22.3 1.3 copy-start.1
  23.5 1.0 copy-start.4
  23.7 1.1 copy-start.2
  26.4 5.8 %copy-start.6 = (pred[192,384]{1,0:T(8,128)(4,1)}, pred[192,384]{1,0:T(8,128)(4,1)S(1)}, u32[]{:S(2)}) copy-start(pred[192,384]{1,0:T(8,128)(4,1)S(1)} %fusion.34) | copy-start | bytes 221188
  26.6 5.7 %copy-start.3 = (bf16[192,256]{0,1:T(8,128)(2,1)}, bf16[192,256]{0,1:T(8,128)(2,1)S(1)}, u32[]{:S(2)}) copy-start(bf16[192,256]{0,1:T(8,128)(2,1)S(1)} %copy.33) | copy-start | bytes 294916
  30.0 0.6 copy-start.15
  31.7 0.6 copy-start.11
  33.0 1.4 copy-start.12
  33.0 1.7 copy-start.5
  34.4 0.9 copy-start.7
  35.2 0.6 copy-start.18
  35.2 0.6 copy-start.22
  35.8 1.4 copy-start.9
  37.2 24.7 %all-to-all-start.1 = ((bf16[32,72,256]{2,1,0:T(8,128)(2,1)}), bf16[32,72,256]{2,1,0:T(8,128)(2,1)S(1)}, u32[]{:S(2)}, u32[]{:S(2)}) async-start(bf16[32,72,256]{2,1,0:T(8,128)(2,1)} %broadcast_in_dim.118), calls=%async_computation.1 | async-start | bytes 2359296 | tf_op jit(solution)/shard_map/all_to_all | solution.py:23
  42.0 95.8 %all-gather.3.cloned.1.call-start = ((), (), s32[]{:S(2)}) async-start(), calls=%async_computation.4 | async-start | bytes 3342336 | tf_op jit(solution)/shard_map/all_gather | solution.py:40
  62.7 2.3 copy-start.19
  64.7 1.0 copy-start.20
  66.9 32.2 %copy-start.21 = (bf16[1024,128]{1,0:T(8,128)(2,1)S(1)}, bf16[1024,128]{1,0:T(8,128)(2,1)}, u32[]{:S(2)}) copy-start(bf16[1024,128]{1,0:T(8,128)(2,1)} %param.20) | copy-start | bytes 786436
  141.0 51.5 %copy-start.8 = (bf16[128,1024]{1,0:T(8,128)(2,1)S(1)}, bf16[128,1024]{1,0:T(8,128)(2,1)}, u32[]{:S(2)}) copy-start(bf16[128,1024]{1,0:T(8,128)(2,1)} %param.23) | copy-start | bytes 786436
  227.4 4.8 %copy-start.16 = (s32[8]{0:T(128)S(1)}, s32[8]{0:T(128)}, u32[]{:S(2)}) copy-start(s32[8]{0:T(128)} %copy-done.15) | copy-start | bytes 100
  227.4 5.4 %copy-start.14 = (s32[256]{0:T(256)S(1)}, s32[256]{0:T(256)}, u32[]{:S(2)}) copy-start(s32[256]{0:T(256)} %copy-done.13) | copy-start | bytes 3076
  227.4 6.1 %copy-start.10 = (bf16[192,4,64]{0,2,1:T(8,128)(2,1)S(1)}, bf16[192,4,64]{0,2,1:T(8,128)(2,1)}, u32[]{:S(2)}) copy-start(bf16[192,4,64]{0,2,1:T(8,128)(2,1)} %copy-done.9) | copy-start | bytes 294916
  227.4 21.1 %all-to-all-start.3 = ((bf16[32,12,1024]{2,1,0:T(8,128)(2,1)}), bf16[32,12,1024]{2,1,0:T(8,128)(2,1)S(1)}, u32[]{:S(2)}, u32[]{:S(2)}) async-start(bf16[32,12,1024]{2,1,0:T(8,128)(2,1)} %broadcast_in_dim.119), calls=%async_computation.3 | async-start | bytes 2097152 | tf_op jit(solution)/shard_map/all_to_all | solution.py:23
Sparse Core Ops, SparseCore 0:
  67.0 70.6 all-gather.2
where the time goes:
time: 258 us; the launch traced here: 257 us
  blocking collectives  62 us (24%)
  waiting for transfers between devices  55.7 us (22%)
  local copies, waits for them, and re-layouts  47.7 us (18%)
  matrix products  32.5 us (13%)
  starting transfers between devices  21.5 us (8%)
  between operations  14.6 us (6%)
  loops' own time  12.5 us (5%)
  other arithmetic  10.6 us (4%)
    all_gather x1, waiting for transfers between devices, sent_together(): filled = lax.all_gather(both, axis, axis=dim, tiled=True)  38.2 us
    all_to_all x1, blocking collectives, sent_and_summed(): lax.all_to_all(tiles, axis, split_axis=0, concat_axis=0, tiled=True)  33 us
    all_gather x1, blocking collectives, per_device(): lax.all_gather(positions, 'bytes', axis=0, tiled=True)  29 us
    dot_general x16, matrix products, attend_block(): jnp.einsum('qhd,khd->hqk', queries_h, keys_s, preferred_element_type=jnp....  18.9 us
    gather x10, local copies, waits for them, and re-layouts, per_device(): jnp.searchsorted(running, targets + 1)  18.9 us
    all_to_all x3, waiting for transfers between devices, copy_for_each(): return lax.all_to_all(copies, axis, split_axis=0, concat_axis=0, tiled=True)  17.5 us
    all_to_all x3, starting transfers between devices, copy_for_each(): return lax.all_to_all(copies, axis, split_axis=0, concat_axis=0, tiled=True)  16.9 us
    another operation x1, loops' own time, per_device(): lax.scan(attend_block, running_state, jnp.arange(span_rows // query_rows,...  11.9 us
  transfers between devices with their start and end apart: 5, of which 3 were waited for; matrix products, arithmetic and copies ran while one was open for 12% of the time, Pallas kernels for 0%

commit v1 on v0

--- a/solution.py
+++ b/solution.py
@@ -10,6 +10,11 @@
 EPSILON = 1e-06
 NEGATIVE = -1e30
 FARAWAY = 1 << 30
+
+
+def gather_from_all(shard, axis, dim):
+    copies = jnp.concatenate([shard] * lax.axis_size(axis), axis=dim)
+    return lax.all_to_all(copies, axis, dim, dim, tiled=True)
 
 
 def from_behind(value, axis, steps):
@@ -161,7 +166,7 @@
     running_state = initial
     keys_p, values_p, places_p = (
         *sent_together((keys_l, values_l), "bytes", 0, 1),
-        lax.all_gather(positions, "bytes", axis=0, tiled=True),
+        gather_from_all(positions, "bytes", 0),
     )
     span_rows = keys_p.shape[0]
 

time: 258 us -> 256 us (level)
  blocking collectives: 62 us -> 32.9 us
  starting transfers between devices: 21.5 us -> 36.1 us
  waiting for transfers between devices: 55.7 us -> 69.7 us
    all_gather x1 -> x0, blocking collectives: 29 us -> none  [per_device(): lax.all_gather(positions, 'bytes', axis=0, tiled=True)]
    all_to_all x0 -> x1, starting transfers between devices: none -> 14.5 us  [gather_from_all(): return lax.all_to_all(copies, axis, dim, dim, tiled=True)]
    all_gather x1, waiting for transfers between devices: 38.2 us -> 52.2 us  [sent_together(): filled = lax.all_gather(both, axis, axis=dim, tiled=True)]
  transfers between devices with their start and end apart: 5 -> 6, of which waited for: 3 -> 3; matrix products, arithmetic and copies ran while one was open for 12% -> 14% of each run, Pallas kernels for 0% -> 0%
where the time goes in v1:
time: 256 us; the launch traced here: 255 us
  waiting for transfers between devices  69.7 us (27%)
  local copies, waits for them, and re-layouts  47 us (18%)
  starting transfers between devices  36.1 us (14%)
  blocking collectives  32.9 us (13%)
  matrix products  32.6 us (13%)
  between operations  14.7 us (6%)
  loops' own time  11.8 us (5%)
  other arithmetic  10.6 us (4%)
    all_gather x1, waiting for transfers between devices, sent_together(): filled = lax.all_gather(both, axis, axis=dim, tiled=True)  52.2 us
    all_to_all x1, blocking collectives, sent_and_summed(): lax.all_to_all(tiles, axis, split_axis=0, concat_axis=0, tiled=True)  32.9 us
    dot_general x16, matrix products, attend_block(): jnp.einsum('qhd,khd->hqk', queries_h, keys_s, preferred_element_type=jnp....  18.9 us
    gather x10, local copies, waits for them, and re-layouts, per_device(): jnp.searchsorted(running, targets + 1)  18.9 us
    all_to_all x3, waiting for transfers between devices, copy_for_each(): return lax.all_to_all(copies, axis, split_axis=0, concat_axis=0, tiled=True)  17.5 us
    all_to_all x3, starting transfers between devices, copy_for_each(): return lax.all_to_all(copies, axis, split_axis=0, concat_axis=0, tiled=True)  16.9 us
    all_to_all x1, starting transfers between devices, gather_from_all(): return lax.all_to_all(copies, axis, dim, dim, tiled=True)  14.5 us
    another operation x1, loops' own time, per_device(): lax.scan(attend_block, running_state, jnp.arange(span_rows // query_rows,...  11.2 us
  transfers between devices with their start and end apart: 6, of which 3 were waited for; matrix products, arithmetic and copies ran while one was open for 14% of the time, Pallas kernels for 0%

profile of v1, /device:TPU:1, one launch (start us, length us, event | category | flops | bytes accessed | tf_op | source)
XLA Modules:
  0.0 255.2 jit_solution(12983609631383623301)
XLA Ops:
  6.5 4.6 %collective-permute-start = (s32[192]{0:T(256)}, s32[192]{0:T(256)S(1)}, u32[]{:S(2)}, u32[]{:S(2)}) collective-permute-start(s32[192]{0:T(256)} %param.14), channel_id=1, source_target_pairs={{0,4},{4,8},{8,12},{12,16},{16,20},{20,24},{24,28},{28,32},{32,36}... | collective-permute-start | bytes 2312 | tf_op jit(solution)/shard_map/ppermute | solution.py:23
  11.2 0.7 broadcast_compare_fusion.1
  14.3 0.6 broadcast_in_dim.111
  14.9 7.3 %all-to-all-start = ((s32[32,1,1]{2,1,0:T(1,128)}), s32[32,1,1]{2,1,0:T(1,128)S(1)}, u32[]{:S(2)}, u32[]{:S(2)}) async-start(s32[32,1,1]{2,1,0:T(1,128)} %broadcast_in_dim.111), calls=%async_computation | async-start | bytes 32768 | tf_op jit(solution)/shard_map/all_to_all | solution.py:28
  22.3 1.1 multiply_reduce_fusion
  24.8 0.9 convolution_convert_fusion.7
  26.6 2.6 %all-to-all-done = s32[32,1,1]{2,1,0:T(1,128)S(1)} async-done(((s32[32,1,1]{2,1,0:T(1,128)}), s32[32,1,1]{2,1,0:T(1,128)S(1)}, u32[]{:S(2)}, u32[]{:S(2)}) %all-to-all-start) | async-done | bytes 160 | tf_op jit(solution)/shard_map/all_to_all | solution.py:28
  29.1 0.7 reduce.8
  32.2 0.7 fusion.53
  33.0 1.3 fusion.25
  36.1 1.1 broadcast_in_dim.118
  37.2 4.8 %all-to-all-start.2 = ((bf16[32,72,256]{2,1,0:T(8,128)(2,1)}), bf16[32,72,256]{2,1,0:T(8,128)(2,1)S(1)}, u32[]{:S(2)}, u32[]{:S(2)}) async-start(bf16[32,72,256]{2,1,0:T(8,128)(2,1)} %broadcast_in_dim.118), calls=%async_computation.2 | async-start | bytes 2359296 | tf_op jit(solution)/shard_map/all_to_all | solution.py:28
  42.0 19.8 %while.39 = (s32[]{:T(128)}, u32[384]{0:T(512)S(1)}, u32[384]{0:T(512)S(1)}, s32[576]{0:T(1024)S(1)}, s32[]{:T(128)}, /*index=5*/s32[]{:T(128)}, s32[]{}) while((s32[]{:T(128)}, u32[384]{0:T(512)S(1)}, u32[384]{0:T(512)S(1)}, s32[576]{0:T(1024)S(1)}, s32[]{:T(128)}, /*index=5*/s32[]{:T(128)}, s32[]{}) %tuple.72), condition=%wide.region_10.11_spmd.clone, body=%wide.region_9.10_spmd.clone.sunk | while | flops 8324 | bytes 29541 | solution.py:151
  42.1 1.9 gather_fusion
  44.1 1.9 gather_fusion
  46.0 1.9 gather_fusion
  48.0 1.9 gather_fusion
  50.0 1.9 gather_fusion
  52.0 1.9 gather_fusion
  54.0 1.9 gather_fusion
  56.0 1.9 gather_fusion
  57.9 1.9 gather_fusion
  59.9 1.9 gather_fusion
  62.7 2.1 gather_fusion.2
  66.2 0.7 pad_maximum_fusion.2
  66.9 1.9 gather_fusion.1
  69.4 0.6 fusion.42
  70.1 0.6 concatenate.15
  70.7 14.5 %all-to-all-start.1 = ((s32[16,384,1]{1,2,0:T(1,128)}), s32[16,384,1]{1,2,0:T(1,128)S(1)}, u32[]{:S(2)}, u32[]{:S(2)}) async-start(s32[16,384,1]{1,2,0:T(1,128)} %concatenate.15), calls=%async_computation.1 | async-start | bytes 49152 | tf_op jit(solution)/shard_map/all_to_all | solution.py:17
  85.7 52.2 %all-gather.2.cloned.1.call-done = bf16[6144,256]{0,1:T(8,128)(2,1)} async-done(((bf16[384,256]{0,1:T(8,128)(2,1)}), bf16[6144,256]{0,1:T(8,128)(2,1)}) %all-gather.2.cloned.1.call-update) | async-done | bytes 3145744 | tf_op jit(solution)/shard_map/all_gather | solution.py:45
  137.9 3.3 %fusion.52 = (bf16[6144,128]{0,1:T(8,128)(2,1)S(1)}, bf16[6144,128]{0,1:T(8,128)(2,1)}) fusion(bf16[6144,256]{0,1:T(8,128)(2,1)} %all-gather.2.cloned.1.call-done), kind=kLoop, calls=%fused_computation.120 | loop fusion | bytes 6291456 | tf_op jit(solution)/shard_map/split | solution.py:46
  141.1 49.5 %while.40 = (s32[]{:T(128)}, f32[1,384]{1,0:T(1,128)S(1)}, f32[1,384]{1,0:T(1,128)S(1)}, f32[384,1,128]{0,2,1:T(8,128)S(1)}, s32[16]{0:T(128)S(1)}, /*index=5*/s...) while((s32[]{:T(128)}, f32[1,384]{1,0:T(1,128)S(1)}, ...), condition=%wide.region_15.16_spmd.clone, body=%wide.region_12.15_spmd.clone.sunk | while | flops 77416712 | bytes 2498263 | solution.py:201
  141.2 0.6 dynamic_slice.34
  142.5 1.2 fusion.84
  144.2 0.6 dynamic_slice.34
  145.6 1.2 fusion.84
  147.3 0.6 dynamic_slice.34
  148.7 1.2 fusion.84
  150.4 0.6 dynamic_slice.34
  151.8 1.2 fusion.84
  153.5 0.6 dynamic_slice.34
  154.9 1.2 fusion.84
  156.6 0.6 dynamic_slice.34
  157.9 1.2 fusion.84
  159.7 0.6 dynamic_slice.34
  161.0 1.2 fusion.84
  162.8 0.6 dynamic_slice.34
  164.1 1.2 fusion.84
  167.2 1.2 fusion.84
  170.3 1.2 fusion.84
  173.4 1.2 fusion.84
  176.5 1.2 fusion.84
  179.6 1.2 fusion.84
  182.7 1.2 fusion.84
  185.8 1.2 fusion.84
  188.9 1.2 fusion.84
  191.3 32.9 %all_to_all.30 = bf16[32,12,1024]{2,1,0:T(8,128)(2,1)S(1)} all-to-all(bf16[32,12,1024]{2,1,0:T(8,128)(2,1)S(1)} %reshape.271), channel_id=1, replica_groups=mesh['bytes'=16,'ctx'=8,'tp'=4] {'ctx','tp'}, dimensions={0} | all-to-all | bytes 1572864 | tf_op jit(solution)/shard_map/all_to_all | solution.py:56
  224.4 1.1 broadcast_in_dim.119
  225.5 4.8 %all-to-all-start.4 = ((bf16[32,12,1024]{2,1,0:T(8,128)(2,1)}), bf16[32,12,1024]{2,1,0:T(8,128)(2,1)S(1)}, u32[]{:S(2)}, u32[]{:S(2)}) async-start(bf16[32,12,1024]{2,1,0:T(8,128)(2,1)} %broadcast_in_dim.119), calls=%async_computation.4 | async-start | bytes 2097152 | tf_op jit(solution)/shard_map/all_to_all | solution.py:28
  230.3 0.6 fusion.44
  230.9 0.7 compare_select_fusion.3
  231.7 14.9 %all-to-all-done.4 = bf16[32,12,1024]{2,1,0:T(8,128)(2,1)S(1)} async-done(((bf16[32,12,1024]{2,1,0:T(8,128)(2,1)}), bf16[32,12,1024]{2,1,0:T(8,128)(2,1)S(1)}, u32[]{:S(2)}, u32[]{:S(2)}) %all-to-all-start.4) | async-done | bytes 786464 | tf_op jit(solution)/shard_map/all_to_all | solution.py:28
  246.8 0.9 gather_fusion.3
  247.7 0.7 add_convert_fusion
  (269 shorter events, 27.4 us)
Async XLA Ops:
  6.5 15.8 %copy-start = (bf16[256,1024]{1,0:T(8,128)(2,1)S(1)}, bf16[256,1024]{1,0:T(8,128)(2,1)}, u32[]{:S(2)}) copy-start(bf16[256,1024]{1,0:T(8,128)(2,1)} %param.16) | copy-start | bytes 1572868
  6.5 24.7 %collective-permute-start = (s32[192]{0:T(256)}, s32[192]{0:T(256)S(1)}, u32[]{:S(2)}, u32[]{:S(2)}) collective-permute-start(s32[192]{0:T(256)} %param.14), channel_id=1, source_target_pairs={{0,4},{4,8},{8,12},{12,16},{16,20},{20,24},{24,28},{28,32},{32,36}... | collective-permute-start | bytes 2312 | tf_op jit(solution)/shard_map/ppermute | solution.py:23
  12.5 0.6 copy-start.13
  13.1 10.4 %copy-start.17 = (s32[192]{0:T(256)}, s32[192]{0:T(256)S(1)}, u32[]{:S(2)}) copy-start(s32[192]{0:T(256)S(1)} %slice_add_fusion) | copy-start | bytes 2308
  14.9 14.2 %all-to-all-start = ((s32[32,1,1]{2,1,0:T(1,128)}), s32[32,1,1]{2,1,0:T(1,128)S(1)}, u32[]{:S(2)}, u32[]{:S(2)}) async-start(s32[32,1,1]{2,1,0:T(1,128)} %broadcast_in_dim.111), calls=%async_computation | async-start | bytes 32768 | tf_op jit(solution)/shard_map/all_to_all | solution.py:28
  22.3 1.3 copy-start.1
  23.5 1.0 copy-start.4
  23.7 1.1 copy-start.2
  26.4 5.8 %copy-start.6 = (pred[192,384]{1,0:T(8,128)(4,1)}, pred[192,384]{1,0:T(8,128)(4,1)S(1)}, u32[]{:S(2)}) copy-start(pred[192,384]{1,0:T(8,128)(4,1)S(1)} %fusion.34) | copy-start | bytes 221188
  26.6 5.7 %copy-start.3 = (bf16[192,256]{0,1:T(8,128)(2,1)}, bf16[192,256]{0,1:T(8,128)(2,1)S(1)}, u32[]{:S(2)}) copy-start(bf16[192,256]{0,1:T(8,128)(2,1)S(1)} %copy.33) | copy-start | bytes 294916
  30.0 0.6 copy-start.15
  31.7 0.6 copy-start.11
  33.0 1.4 copy-start.12
  33.0 1.7 copy-start.5
  34.4 0.9 copy-start.7
  35.2 0.6 copy-start.18
  35.2 0.6 copy-start.22
  35.8 1.4 copy-start.9
  37.2 24.7 %all-to-all-start.2 = ((bf16[32,72,256]{2,1,0:T(8,128)(2,1)}), bf16[32,72,256]{2,1,0:T(8,128)(2,1)S(1)}, u32[]{:S(2)}, u32[]{:S(2)}) async-start(bf16[32,72,256]{2,1,0:T(8,128)(2,1)} %broadcast_in_dim.118), calls=%async_computation.2 | async-start | bytes 2359296 | tf_op jit(solution)/shard_map/all_to_all | solution.py:28
  42.0 95.9 %all-gather.2.cloned.1.call-start = ((), (), s32[]{:S(2)}) async-start(), calls=%async_computation.5 | async-start | bytes 3342336 | tf_op jit(solution)/shard_map/all_gather | solution.py:45
  62.7 2.3 copy-start.19
  64.7 1.0 copy-start.20
  66.9 18.4 %copy-start.21 = (bf16[1024,128]{1,0:T(8,128)(2,1)S(1)}, bf16[1024,128]{1,0:T(8,128)(2,1)}, u32[]{:S(2)}) copy-start(bf16[1024,128]{1,0:T(8,128)(2,1)} %param.20) | copy-start | bytes 786436
  70.7 70.4 %all-to-all-start.1 = ((s32[16,384,1]{1,2,0:T(1,128)}), s32[16,384,1]{1,2,0:T(1,128)S(1)}, u32[]{:S(2)}, u32[]{:S(2)}) async-start(s32[16,384,1]{1,2,0:T(1,128)} %concatenate.15), calls=%async_computation.1 | async-start | bytes 49152 | tf_op jit(solution)/shard_map/all_to_all | solution.py:17
  141.1 49.5 %copy-start.8 = (bf16[128,1024]{1,0:T(8,128)(2,1)S(1)}, bf16[128,1024]{1,0:T(8,128)(2,1)}, u32[]{:S(2)}) copy-start(bf16[128,1024]{1,0:T(8,128)(2,1)} %param.23) | copy-start | bytes 786436
  225.5 4.8 %copy-start.16 = (s32[8]{0:T(128)S(1)}, s32[8]{0:T(128)}, u32[]{:S(2)}) copy-start(s32[8]{0:T(128)} %copy-done.15) | copy-start | bytes 100
  225.5 5.4 %copy-start.14 = (s32[256]{0:T(256)S(1)}, s32[256]{0:T(256)}, u32[]{:S(2)}) copy-start(s32[256]{0:T(256)} %copy-done.13) | copy-start | bytes 3076
  225.5 6.1 %copy-start.10 = (bf16[192,4,64]{0,2,1:T(8,128)(2,1)S(1)}, bf16[192,4,64]{0,2,1:T(8,128)(2,1)}, u32[]{:S(2)}) copy-start(bf16[192,4,64]{0,2,1:T(8,128)(2,1)} %copy-done.9) | copy-start | bytes 294916
  225.5 21.1 %all-to-all-start.4 = ((bf16[32,12,1024]{2,1,0:T(8,128)(2,1)}), bf16[32,12,1024]{2,1,0:T(8,128)(2,1)S(1)}, u32[]{:S(2)}, u32[]{:S(2)}) async-start(bf16[32,12,1024]{2,1,0:T(8,128)(2,1)} %broadcast_in_dim.119), calls=%async_computation.4 | async-start | bytes 2097152 | tf_op jit(solution)/shard_map/all_to_all | solution.py:28
Sparse Core Ops, SparseCore 0:
  67.0 70.7 all-gather.1
